TPU v7x, 32 devices: a whole 2x2x4 slice. The times are simulated.
32 devices in a mesh: gx: 4 (over y, x), gy: 2 (over core), gz: 4 (over z).
Axes of the slice: x: 2, y: 2, z: 4, core: 2. Of those that a mesh axis runs over, the one named last changes fastest.
Arguments:
- pair_blocks: float32 [529, 1024], P(None, ('gx', 'gy', 'gz')), may hold values from -6 to 6
- basis_map: float32 [529, 64], replicated, may hold values from -0.25 to 0.25
- pair_cells: int32 [3, 1024], P(None, ('gx', 'gy', 'gz')), may hold values from 0 to 511, as said below
- pair_offsets: float32 [3, 1024], P(None, ('gx', 'gy', 'gz')), may hold values from 0 to 1
- exponent_index: int32 [1024], P(('gx', 'gy', 'gz')), may hold values from 0 to 15
- radius_index: int32 [1024], P(('gx', 'gy', 'gz')), may hold values from 0 to 4
- exponents: float32 [16], replicated, may hold values from 7 to 9
Outputs:
- density: float32 [32, 64, 512], P('gx', 'gy', 'gz')
- spectrum: float32 [2, 512, 64, 32], P(None, ('gy', 'gz'), 'gx')
Inputs may be any that keep to these rules, and one draw needn't show every extreme that they name: The y of pair_cells column p lies among the 32 cells, and its z among the 128 cells, of the gy and gz index of the device that holds column p. Of the pairs that one device holds at most 16 have x in the same run of 8 cells that one gx index holds, and in every draw some such run gets exactly 16 from every device.
All inputs are finite; a program needn't handle non-finite values.
Results may differ from a plain program's by a relative error of at most 0.0003.
Values sent between devices are 32-bit elements; how exact they have to be, the bound alone decides.
No kernel may reach another device: no remote copies, remote signals or barrier semaphores. Data moves between devices by JAX's collectives and lax.ppermute only.
A program may use at most 64 MiB of HBM per device.

v0:
```python
import math

import jax
import jax.numpy as jnp
from jax import lax
from jax.sharding import PartitionSpec as P

DEG = 3
HALO = 8
CX = 8
CY = 32
CZ = 128


highest = lax.Precision.HIGHEST


def padded_2(block, sides, width):
    for axis, dim in sides:
        count = lax.axis_size(axis)
        forward = [(i, i + 1) for i in range(count - 1)]
        forward.append((count - 1, 0))
        backward = [(target, source) for source, target in forward]
        low = lax.ppermute(
            lax.slice_in_dim(block, block.shape[dim] - width, None, axis=dim), axis, forward
        )
        high = lax.ppermute(lax.slice_in_dim(block, 0, width, axis=dim), axis, backward)
        block = jnp.concatenate([low, block, high], axis=dim)
    return block


def place_columns(values, slot_ids, slot_count):
    empty = jnp.zeros((values.shape[0], slot_count), values.dtype)
    return empty.at[:, slot_ids].set(values)


def axis_factors(centres, offsets_row, exponent_values, radius_cells, anchor, extent):
    coordinate = anchor - HALO + jnp.arange(extent, dtype=jnp.int32)
    offset_cells = coordinate[None, :] - centres[:, None]
    distance = offset_cells.astype(jnp.float32) - offsets_row[:, None]
    inside = (jnp.abs(offset_cells) <= radius_cells[:, None]).astype(jnp.float32)
    envelope = jnp.exp(-exponent_values[:, None] * distance * distance) * inside
    scaled = distance / HALO
    return jnp.stack([scaled**degree * envelope for degree in range(DEG + 1)], 1)


def add_along(target, start, piece, along_dim):
    index = [slice(None)] * target.ndim
    index[along_dim] = slice(start, start + piece.shape[along_dim])
    return target.at[tuple(index)].add(piece)


def fold_rims(padded, along_dim, interior):
    lower_rim = lax.slice_in_dim(padded, 0, HALO, axis=along_dim)
    middle = lax.slice_in_dim(padded, 2 * HALO, 2 * HALO + interior, axis=along_dim)
    upper_rim = lax.slice_in_dim(padded, interior + 3 * HALO, interior + 4 * HALO, axis=along_dim)
    middle = add_along(middle, 0, lower_rim, along_dim)
    return add_along(middle, interior - HALO, upper_rim, along_dim)


def dft_parts(length):
    indices = jnp.arange(length, dtype=jnp.int32)
    product = indices[:, None] * indices[None, :] % length
    angles = product.astype(jnp.float32) * (2.0 * math.pi / length)
    factor = 1.0 / math.sqrt(length)
    return (jnp.cos(angles) * factor, jnp.sin(angles) * factor)


def shards(
    pair_blocks, basis_map, pair_cells, pair_offsets, exponent_index, radius_index, exponents
):
    pair_dev = pair_blocks.shape[1]
    x_devices = lax.axis_size("gx")
    capacity = 2 * pair_dev // x_devices
    slot_count = x_devices * capacity
    selector = (
        exponent_index[None, :] == jnp.arange(exponents.shape[0], dtype=jnp.int32)[:, None]
    ).astype(jnp.float32)
    radius_own = HALO - radius_index
    radius_float = radius_own.astype(jnp.float32)
    exponent_values = jnp.dot(exponents, selector, precision=highest) / (
        radius_float * radius_float
    )
    owners = pair_cells[0] // CX
    member = (owners[:, None] == jnp.arange(x_devices, dtype=jnp.int32)[None, :]).astype(jnp.int32)
    within = jnp.sum((jnp.cumsum(member, axis=0) - member) * member, axis=1)
    slot_ids = owners * capacity + within
    extras = jnp.concatenate([pair_offsets, exponent_values[None, :]], 0)
    labels = jnp.concatenate([pair_cells, radius_own[None, :]], 0)
    routed_labels = place_columns(labels, slot_ids, slot_count).reshape(4, x_devices, capacity)
    outgoing = place_columns(jnp.concatenate([pair_blocks, extras], 0), slot_ids, slot_count)
    arrived, arrived_labels = (
        lax.all_to_all(
            outgoing.reshape(-1, x_devices, capacity), "gx", split_axis=1, concat_axis=1, tiled=True
        ),
        lax.all_to_all(routed_labels, "gx", split_axis=1, concat_axis=1, tiled=True),
    )
    arrived = arrived.reshape(-1, slot_count)
    pair_coefs = jnp.dot(basis_map.T, arrived[:-4], precision=highest)
    arrived_labels = arrived_labels.reshape(4, slot_count)
    offsets_in = arrived[-4:-1]
    exponent_in = arrived[-1]
    centres = arrived_labels[:3]
    radius_cells = arrived_labels[3]
    extent_x = CX + 2 * HALO
    extent_y = CY + 2 * HALO
    extent_z = CZ + 2 * HALO
    along_x = axis_factors(
        centres[0], offsets_in[0], exponent_in, radius_cells, lax.axis_index("gx") * CX, extent_x
    )
    along_y = axis_factors(
        centres[1], offsets_in[1], exponent_in, radius_cells, lax.axis_index("gy") * CY, extent_y
    )
    along_z = axis_factors(
        centres[2], offsets_in[2], exponent_in, radius_cells, lax.axis_index("gz") * CZ, extent_z
    )
    side = DEG + 1
    coef_cube = pair_coefs.T.reshape(slot_count, side, side, side)
    partial_z = jnp.einsum("sijk,skc->sijc", coef_cube, along_z, precision=highest)
    plane_groups = jnp.transpose(along_x.reshape(slot_count, side, extent_x // 8, 8), (2, 0, 1, 3))

    def planes(group_x):
        mixed_planes = jnp.einsum("sia,sijc->sjac", group_x, partial_z, precision=highest)
        return jnp.einsum("sjb,sjac->abc", along_y, mixed_planes, precision=highest)

    extended = lax.map(planes, plane_groups).reshape(extent_x, extent_y, extent_z)
    padded = padded_2(extended, (("gx", 0), ("gy", 1), ("gz", 2)), HALO)
    density = fold_rims(fold_rims(fold_rims(padded, 0, CX), 1, CY), 2, CZ)
    depth_local = lax.all_to_all(density, "gz", split_axis=1, concat_axis=2, tiled=True)
    depth_size = depth_local.shape[2]
    cosine_z, sine_z = dft_parts(depth_size)
    real_z = jnp.einsum("xyz,zk->xyk", depth_local, cosine_z, precision=highest)
    imag_z = -jnp.einsum("xyz,zk->xyk", depth_local, sine_z, precision=highest)
    section_z = jnp.stack([real_z, imag_z])
    rows_devices = lax.axis_size("gy")
    depth_devices = lax.axis_size("gz")
    depth_piece = depth_size // (rows_devices * depth_devices)
    split_view = section_z.reshape(
        2, CX, 1, 1, section_z.shape[2], rows_devices, depth_devices, depth_piece
    )
    moved_rows = lax.all_to_all(
        lax.all_to_all(split_view, "gy", split_axis=5, concat_axis=2, tiled=True),
        "gz",
        split_axis=6,
        concat_axis=3,
        tiled=True,
    )
    rows_local = moved_rows.reshape(2, CX, -1, depth_piece)
    cosine_y, sine_y = dft_parts(rows_local.shape[2])
    real_in = rows_local[0]
    imag_in = rows_local[1]
    real_y = jnp.einsum("xyk,yl->klx", real_in, cosine_y, precision=highest) + jnp.einsum(
        "xyk,yl->klx", imag_in, sine_y, precision=highest
    )
    imag_y = jnp.einsum("xyk,yl->klx", imag_in, cosine_y, precision=highest) - jnp.einsum(
        "xyk,yl->klx", real_in, sine_y, precision=highest
    )
    section_y = jnp.stack([real_y, imag_y])
    width_local = lax.all_to_all(section_y, "gx", split_axis=2, concat_axis=3, tiled=True)
    cosine_x, sine_x = dft_parts(width_local.shape[3])
    real_w = width_local[0]
    imag_w = width_local[1]
    real_x = jnp.einsum("kyx,xm->kym", real_w, cosine_x, precision=highest) + jnp.einsum(
        "kyx,xm->kym", imag_w, sine_x, precision=highest
    )
    imag_x = jnp.einsum("kyx,xm->kym", imag_w, cosine_x, precision=highest) - jnp.einsum(
        "kyx,xm->kym", real_w, sine_x, precision=highest
    )
    spectrum = jnp.stack([real_x, imag_x])
    return (density, spectrum)


def solution(mesh):
    placed = (
        P(None, ("gx", "gy", "gz")),
        P(),
        P(None, ("gx", "gy", "gz")),
        P(None, ("gx", "gy", "gz")),
        P(("gx", "gy", "gz")),
        P(("gx", "gy", "gz")),
        P(),
    )
    return jax.shard_map(
        shards,
        mesh=mesh,
        in_specs=placed,
        out_specs=(P("gx", "gy", "gz"), P(None, ("gy", "gz"), "gx", None)),
        check_vma=False,
    )
```

profile of v0, /device:TPU:0, one launch (start us, length us, event | category | flops | bytes accessed | tf_op | source)
XLA Modules:
  0.0 139.2 jit_solution(2050929000422461326)
XLA Ops:
  0.6 0.7 and_select_fusion
  1.7 0.7 fusion.121
  3.0 0.7 add_bitcast_fusion
  4.5 0.7 copy.77
  5.2 5.2 %all-to-all-start = ((s32[4,4,16]{2,0,1:T(4,128)}), s32[4,4,16]{2,0,1:T(4,128)S(1)}, u32[]{:S(2)}, u32[]{:S(2)}) async-start(s32[4,4,16]{2,0,1:T(4,128)} %copy.77), calls=%async_computation | async-start | bytes 16384 | tf_op jit(solution)/shard_map/all_to_all | solution.py:96
  10.4 0.8 fusion.15
  11.3 0.8 copy.78
  12.0 1.0 dot_general.53
  13.0 1.8 %scatter_custom_fusion.1 = f32[533,64]{0,1:T(8,128)} fusion(s32[32]{0:T(128)S(1)} %fusion.121, f32[1,32]{0,1:T(8,128)S(1)} %copy.79, f32[]{:T(128)} %constant.310, f32[3,32]{0,1:T(8,128)S(1)} %copy.78, f32[529,32]{0,1:T(8,128)} %param.25, f32[]{:T(128)} %constant.271.clone.1), kind=kCustom, calls=%fused_computation.89 | custom fusion | flops 34112 | bytes 236936 | tf_op jit(solution)/shard_map/scatter | solution.py:34
  15.1 3.9 %all-to-all-start.1 = ((f32[533,4,16]{0,2,1:T(8,128)}), f32[533,4,16]{0,2,1:T(8,128)S(1)}, u32[]{:S(2)}, u32[]{:S(2)}) async-start(f32[533,4,16]{0,2,1:T(8,128)} %bitcast.20), calls=%async_computation.1 | async-start | bytes 327680 | tf_op jit(solution)/shard_map/all_to_all | solution.py:93
  19.3 4.7 %all-to-all-done.1 = f32[533,4,16]{0,2,1:T(8,128)S(1)} async-done(((f32[533,4,16]{0,2,1:T(8,128)}), f32[533,4,16]{0,2,1:T(8,128)S(1)}, u32[]{:S(2)}, u32[]{:S(2)}) %all-to-all-start.1) | async-done | bytes 136480 | tf_op jit(solution)/shard_map/all_to_all | solution.py:93
  25.6 1.5 %fusion.41 = f32[64,4,4,144]{3,1,2,0:T(4,128)S(1)} fusion(f32[64,4,4,4]{3,1,2,0:T(4,128)S(1)} %copy.100, f32[64,4,144,1]{2,0,1,3:T(8,128)S(1)} %maximum_bitcast_fusion), kind=kOutput, calls=%fused_computation.72 | convolution fusion | flops 7077888 | bytes 753664 | tf_op jit(solution)/shard_map/sijk,skc->sijc/dot_general | solution.py:119
  27.4 15.3 %while.18 = (s32[]{:T(128)}, f32[3,8,48,144]{3,2,1,0:T(8,128)S(1)}, f32[3,64,4,8]{1,3,0,2:T(8,128)S(1)}, f32[64,4,4,144]{3,1,2,0:T(4,128)S(1)}, f32[64,4,48]{0,2,1:T(8,128)S(1)}, /*index=5*/s32[]{:T(128)}) while((s32[]{:T(128)}, f32[3,8,48,144]{3,2,1,0:T(8,128)S(1)}, f32[3,64,4,8]{1,3,0,2:T(8,128)S(1)}, f32[64,4,4,144]{3,1,2,0:T(4,128)S(1)}, ...), condition=%wide.region_5.6_spmd, body=%wide.region_4.5_spmd.sunk | while | flops 184025088 | bytes 4399181 | solution.py:126
  27.5 2.3 %convolution_bitcast_fusion.4 = f32[64,4,8,144]{3,2,1,0:T(8,128)S(1)} fusion(f32[64,4,4,144]{3,1,2,0:T(4,128)S(1)} %get-tuple-element.224, f32[1,64,4,8]{3,2,1,0:T(4,128)S(1)} %copy.133), kind=kOutput, calls=%fused_computation.4.clone.1 | convolution fusion | flops 14155776 | bytes 1777664 | tf_op jit(solution)/shard_map/while/body/eval_jaxpr/sia,sijc->sjac/dot_general | solution.py:123
  29.8 2.7 %fusion.189 = f32[3,8,48,144]{3,2,1,0:T(8,128)S(1)} fusion(f32[3,8,48,144]{3,2,1,0:T(8,128)S(1)} %get-tuple-element.216, s32[]{:T(128)} %get-tuple-element.215, f32[64,4,8,144]{3,2,1,0:T(8,128)S(1)} %convolution_bitcast_fusion.4, f32[64,4,48]{0,2,1:T(8,128)S(1)} %get-tuple-element.225), kind=kOutput, calls=%fused_computation.6.clone.1 | convolution fusion | flops 169869312 | bytes 2588676 | tf_op jit(solution)/shard_map/while/body/eval_jaxpr/sjb,sjac->abc/dot_general | solution.py:124
  32.6 2.3 %convolution_bitcast_fusion.4 = f32[64,4,8,144]{3,2,1,0:T(8,128)S(1)} fusion(f32[64,4,4,144]{3,1,2,0:T(4,128)S(1)} %get-tuple-element.224, f32[1,64,4,8]{3,2,1,0:T(4,128)S(1)} %copy.133), kind=kOutput, calls=%fused_computation.4.clone.1 | convolution fusion | flops 14155776 | bytes 1777664 | tf_op jit(solution)/shard_map/while/body/eval_jaxpr/sia,sijc->sjac/dot_general | solution.py:123
  34.9 2.7 %fusion.189 = f32[3,8,48,144]{3,2,1,0:T(8,128)S(1)} fusion(f32[3,8,48,144]{3,2,1,0:T(8,128)S(1)} %get-tuple-element.216, s32[]{:T(128)} %get-tuple-element.215, f32[64,4,8,144]{3,2,1,0:T(8,128)S(1)} %convolution_bitcast_fusion.4, f32[64,4,48]{0,2,1:T(8,128)S(1)} %get-tuple-element.225), kind=kOutput, calls=%fused_computation.6.clone.1 | convolution fusion | flops 169869312 | bytes 2588676 | tf_op jit(solution)/shard_map/while/body/eval_jaxpr/sjb,sjac->abc/dot_general | solution.py:124
  37.7 2.3 %convolution_bitcast_fusion.4 = f32[64,4,8,144]{3,2,1,0:T(8,128)S(1)} fusion(f32[64,4,4,144]{3,1,2,0:T(4,128)S(1)} %get-tuple-element.224, f32[1,64,4,8]{3,2,1,0:T(4,128)S(1)} %copy.133), kind=kOutput, calls=%fused_computation.4.clone.1 | convolution fusion | flops 14155776 | bytes 1777664 | tf_op jit(solution)/shard_map/while/body/eval_jaxpr/sia,sijc->sjac/dot_general | solution.py:123
  40.0 2.7 %fusion.189 = f32[3,8,48,144]{3,2,1,0:T(8,128)S(1)} fusion(f32[3,8,48,144]{3,2,1,0:T(8,128)S(1)} %get-tuple-element.216, s32[]{:T(128)} %get-tuple-element.215, f32[64,4,8,144]{3,2,1,0:T(8,128)S(1)} %convolution_bitcast_fusion.4, f32[64,4,48]{0,2,1:T(8,128)S(1)} %get-tuple-element.225), kind=kOutput, calls=%fused_computation.6.clone.1 | convolution fusion | flops 169869312 | bytes 2588676 | tf_op jit(solution)/shard_map/while/body/eval_jaxpr/sjb,sjac->abc/dot_general | solution.py:124
  42.7 1.1 collective-permute-start
  43.8 1.9 %collective-permute-start.1 = (f32[8,48,144]{2,1,0:T(8,128)S(1)}, f32[8,48,144]{2,1,0:T(8,128)S(1)}, u32[]{:S(2)}, u32[]{:S(2)}) collective-permute-start(f32[8,48,144]{2,1,0:T(8,128)S(1)} %get-tuple-element.163), channel_id=1, source_target_pairs={{8,0},{16,8},{24,16},{0,24},{9,1},{17,9},{25,17},{1,25},{10,2},{18... | collective-permute-start | bytes 663560 | tf_op jit(solution)/shard_map/ppermute | solution.py:27
  45.7 10.0 %collective-permute-done = f32[8,48,144]{2,1,0:T(8,128)S(1)} collective-permute-done((f32[8,48,144]{2,1,0:T(8,128)S(1)}, f32[8,48,144]{2,1,0:T(8,128)S(1)}, u32[]{:S(2)}, u32[]{:S(2)}) %collective-permute-start) | collective-permute-done | bytes 221216 | tf_op jit(solution)/shard_map/ppermute | solution.py:24
  55.7 5.1 %collective-permute-done.1 = f32[8,48,144]{2,1,0:T(8,128)S(1)} collective-permute-done((f32[8,48,144]{2,1,0:T(8,128)S(1)}, f32[8,48,144]{2,1,0:T(8,128)S(1)}, u32[]{:S(2)}, u32[]{:S(2)}) %collective-permute-start.1) | collective-permute-done | bytes 221216 | tf_op jit(solution)/shard_map/ppermute | solution.py:27
  61.4 1.1 collective-permute-done.2
  63.7 1.5 %fusion.168 = (f32[40,64,8]{2,1,0:T(8,128)}, f32[40,64,8]{2,1,0:T(8,128)S(1)}) fusion(f32[40,64,144]{2,1,0:T(8,128)S(1)} %pad_maximum_fusion), kind=kLoop, calls=%fused_computation.252 | loop fusion | bytes 327680 | tf_op jit(solution)/shard_map/slice | solution.py:25
  65.3 1.7 %copy.84 = f32[40,64,8]{1,2,0:T(8,128)S(1)} copy(f32[40,64,8]{2,1,0:T(8,128)} %get-tuple-element.158) | data formatting | bytes 163840 | tf_op jit(solution)/shard_map/slice | solution.py:25
  67.0 1.6 %collective-permute-start.4 = (f32[40,64,8]{1,2,0:T(8,128)S(1)}, f32[40,64,8]{1,2,0:T(8,128)}, u32[]{:S(2)}, u32[]{:S(2)}) collective-permute-start(f32[40,64,8]{1,2,0:T(8,128)S(1)} %copy.84), channel_id=1, source_target_pairs={{0,1},{1,2},{2,3},{3,0},{4,5},{5,6},{6,7},{7,4},{8,9},{9,10},{10,1... | collective-permute-start | bytes 245768 | tf_op jit(solution)/shard_map/ppermute | solution.py:24
  68.6 1.0 copy.85
  69.6 2.2 %collective-permute-start.5 = (f32[40,64,8]{1,2,0:T(8,128)}, f32[40,64,8]{1,2,0:T(8,128)}, u32[]{:S(2)}, u32[]{:S(2)}) collective-permute-start(f32[40,64,8]{1,2,0:T(8,128)} %copy.85), channel_id=1, source_target_pairs={{1,0},{2,1},{3,2},{0,3},{5,4},{6,5},{7,6},{4,7},{9,8},{10,9},{11,1... | collective-permute-start | bytes 245768 | tf_op jit(solution)/shard_map/ppermute | solution.py:27
  71.9 4.0 %collective-permute-done.4 = f32[40,64,8]{1,2,0:T(8,128)} collective-permute-done((f32[40,64,8]{1,2,0:T(8,128)S(1)}, f32[40,64,8]{1,2,0:T(8,128)}, u32[]{:S(2)}, u32[]{:S(2)}) %collective-permute-start.4) | collective-permute-done | bytes 81952 | tf_op jit(solution)/shard_map/ppermute | solution.py:24
  76.0 1.3 copy.86
  77.3 1.4 %collective-permute-done.5 = f32[40,64,8]{1,2,0:T(8,128)} collective-permute-done((f32[40,64,8]{1,2,0:T(8,128)}, f32[40,64,8]{1,2,0:T(8,128)}, u32[]{:S(2)}, u32[]{:S(2)}) %collective-permute-start.5) | collective-permute-done | bytes 81952 | tf_op jit(solution)/shard_map/ppermute | solution.py:27
  78.7 2.4 %copy.87 = f32[40,64,8]{2,1,0:T(8,128)} copy(f32[40,64,8]{1,2,0:T(8,128)} %collective-permute-done.5) | data formatting | bytes 163840 | tf_op jit(solution)/shard_map/ppermute | solution.py:27
  81.1 1.9 %fusion.35 = f32[8,64,160]{2,1,0:T(8,128)S(1)} fusion(f32[40,64,8]{2,1,0:T(8,128)} %copy.87, f32[40,64,8]{2,1,0:T(8,128)S(1)} %copy.86, f32[40,8,144]{2,1,0:T(8,128)} %copy-done.2, f32[40,8,144]{2,1,0:T(8,128)} %copy-done.1, f32[8,48,144]{2,1,0:T(8,128)S(1)} %collective-permute-done.1, f32[24,48,144]{2,1,0:T(8,128)S(1)} %bitcast.191, ...), kind=kLoop, calls=%fused_computation.48 | loop fusion | flops 1638400 | bytes 1966080 | tf_op jit(solution)/shard_map/add | solution.py:50
  83.7 1.5 %scatter-add.19 = f32[8,32,128]{2,1,0:T(8,128)S(1)} dynamic-update-slice(f32[8,32,128]{2,1,0:T(8,128)S(1)} %scatter-add.16, f32[8,32,8]{2,1,0:T(8,128)S(1)} %slice_add_fusion, s32[]{:T(128)} %constant.270.clone.1, s32[]{:T(128)} %constant.270.clone.1, s32[]{:T(128)} %constant.287.clone.1) | dynamic-update-slice | bytes 16388 | tf_op jit(solution)/shard_map/scatter-add | solution.py:50
  85.2 0.7 copy.88
  86.0 4.4 %all-to-all-start.2 = ((f32[8,32,128]{2,0,1:T(8,128)}), f32[8,32,128]{2,0,1:T(8,128)S(1)}, u32[]{:S(2)}, u32[]{:S(2)}) async-start(f32[8,32,128]{2,0,1:T(8,128)} %copy.88), calls=%async_computation.2 | async-start | bytes 262144 | tf_op jit(solution)/shard_map/all_to_all | solution.py:129
  90.3 3.9 %fusion.20 = f32[512,512]{1,0:T(8,128)S(1)} fusion(s32[512]{0:T(512)S(1)} %mul.505), kind=kLoop, calls=%fused_computation.34 | loop fusion | flops 3932160 | bytes 1050624 | tf_op jit(solution)/shard_map/mul | solution.py:66
  94.2 2.0 %all-to-all-done.2 = f32[8,32,128]{2,0,1:T(8,128)S(1)} async-done(((f32[8,32,128]{2,0,1:T(8,128)}), f32[8,32,128]{2,0,1:T(8,128)S(1)}, u32[]{:S(2)}, u32[]{:S(2)}) %all-to-all-start.2) | async-done | bytes 131104 | tf_op jit(solution)/shard_map/all_to_all | solution.py:129
  96.2 4.8 %convolution_negate_fusion = f32[8,8,512]{2,1,0:T(8,128)S(1)} fusion(f32[8,4,8,128]{3,0,2,1:T(8,128)S(1)} %bitcast.204), kind=kOutput, calls=%fused_computation.26 | convolution fusion | flops 205291520 | bytes 262144 | tf_op jit(solution)/shard_map/xyz,zk->xyk/dot_general | solution.py:133
  101.0 1.7 %convolution_bitcast_fusion.1 = f32[1,8,1,1,8,2,4,64]{7,4,6,5,1,3,2,0:T(8,128)S(1)} fusion(f32[2,4,64,512,1]{3,2,1,0,4:T(8,128)S(1)} %bitcast.196, f32[8,4,8,128]{3,0,2,1:T(8,128)S(1)} %bitcast.205), kind=kOutput, calls=%fused_computation.25 | convolution fusion | flops 201326592 | bytes 1310720 | tf_op jit(solution)/shard_map/xyz,zk->xyk/dot_general | solution.py:132
  103.3 3.9 %all_to_all.73 = f32[2,1,32768]{2,1,0:T(1,128)S(1)} all-to-all(f32[2,1,32768]{2,1,0:T(1,128)S(1)} %reshape.1719), channel_id=1, replica_groups=mesh['gx'=4,'gy'=2,'gz'=4] {'gy'}, dimensions={0} | all-to-all | bytes 524288 | tf_op jit(solution)/shard_map/all_to_all | solution.py:142
  107.7 1.5 %reduce.36 = f32[2,32768]{1,0:T(2,128)S(1)} reduce(f32[2,1,32768]{2,1,0:T(1,128)S(1)} %all_to_all.73, f32[]{:T(128)} %broadcast.1248), dimensions={1}, to_apply=%all_to_all.57.reduce_sub_computation | reduce | bytes 524292 | tf_op jit(solution)/shard_map/all_to_all | solution.py:142
  109.9 12.2 %all_to_all.74 = f32[4,1,16384]{2,1,0:T(1,128)S(1)} all-to-all(f32[4,1,16384]{2,1,0:T(1,128)S(1)} %reshape.1721), channel_id=1, replica_groups=mesh['gx'=4,'gy'=2,'gz'=4] {'gz'}, dimensions={0} | all-to-all | bytes 524288 | tf_op jit(solution)/shard_map/all_to_all | solution.py:141
  122.1 1.4 reduce.37
  126.7 8.1 %all_to_all.75 = f32[4,1,16384]{2,1,0:T(1,128)S(1)} all-to-all(f32[4,1,16384]{2,1,0:T(1,128)S(1)} %reshape.1723), channel_id=1, replica_groups=mesh['gx'=4,'gy'=2,'gz'=4] {'gx'}, dimensions={0} | all-to-all | bytes 524288 | tf_op jit(solution)/shard_map/all_to_all | solution.py:159
  134.8 1.4 reduce.38
  138.4 0.8 pad_maximum_fusion.9
  (85 shorter events, 14.2 us)
Async XLA Ops:
  0.6 9.8 %copy-start = (f32[16]{0:T(128)S(1)}, f32[16]{0:T(128)}, u32[]{:S(2)}) copy-start(f32[16]{0:T(128)} %param.31) | copy-start | bytes 196
  5.2 9.9 %all-to-all-start = ((s32[4,4,16]{2,0,1:T(4,128)}), s32[4,4,16]{2,0,1:T(4,128)S(1)}, u32[]{:S(2)}, u32[]{:S(2)}) async-start(s32[4,4,16]{2,0,1:T(4,128)} %copy.77), calls=%async_computation | async-start | bytes 16384 | tf_op jit(solution)/shard_map/all_to_all | solution.py:96
  15.1 9.0 %all-to-all-start.1 = ((f32[533,4,16]{0,2,1:T(8,128)}), f32[533,4,16]{0,2,1:T(8,128)S(1)}, u32[]{:S(2)}, u32[]{:S(2)}) async-start(f32[533,4,16]{0,2,1:T(8,128)} %bitcast.20), calls=%async_computation.1 | async-start | bytes 327680 | tf_op jit(solution)/shard_map/all_to_all | solution.py:93
  42.7 12.9 %collective-permute-start = (f32[8,48,144]{2,1,0:T(8,128)S(1)}, f32[8,48,144]{2,1,0:T(8,128)S(1)}, u32[]{:S(2)}, u32[]{:S(2)}) collective-permute-start(f32[8,48,144]{2,1,0:T(8,128)S(1)} %get-tuple-element.162), channel_id=1, source_target_pairs={{0,8},{8,16},{16,24},{24,0},{1,9},{9,17},{17,25},{25,1},{2,10},{10... | collective-permute-start | bytes 663560 | tf_op jit(solution)/shard_map/ppermute | solution.py:24
  43.8 17.0 %collective-permute-start.1 = (f32[8,48,144]{2,1,0:T(8,128)S(1)}, f32[8,48,144]{2,1,0:T(8,128)S(1)}, u32[]{:S(2)}, u32[]{:S(2)}) collective-permute-start(f32[8,48,144]{2,1,0:T(8,128)S(1)} %get-tuple-element.163), channel_id=1, source_target_pairs={{8,0},{16,8},{24,16},{0,24},{9,1},{17,9},{25,17},{1,25},{10,2},{18... | collective-permute-start | bytes 663560 | tf_op jit(solution)/shard_map/ppermute | solution.py:27
  60.8 1.7 %collective-permute-start.2 = (f32[40,8,144]{2,1,0:T(8,128)S(1)}, f32[40,8,144]{2,1,0:T(8,128)S(1)}, u32[]{:S(2)}, u32[]{:S(2)}) collective-permute-start(f32[40,8,144]{2,1,0:T(8,128)S(1)} %get-tuple-element.160), channel_id=1, source_target_pairs={{0,4},{4,0},{1,5},{5,1},{2,6},{6,2},{3,7},{7,3},{8,12},{12,8},{9,1... | collective-permute-start | bytes 552968 | tf_op jit(solution)/shard_map/ppermute | solution.py:24
  60.9 2.1 %collective-permute-start.3 = (f32[40,8,144]{2,1,0:T(8,128)S(1)}, f32[40,8,144]{2,1,0:T(8,128)S(1)}, u32[]{:S(2)}, u32[]{:S(2)}) collective-permute-start(f32[40,8,144]{2,1,0:T(8,128)S(1)} %get-tuple-element.161), channel_id=1, source_target_pairs={{4,0},{0,4},{5,1},{1,5},{6,2},{2,6},{7,3},{3,7},{12,8},{8,12},{13,... | collective-permute-start | bytes 552968 | tf_op jit(solution)/shard_map/ppermute | solution.py:27
  62.5 2.7 %copy-start.1 = (f32[40,8,144]{2,1,0:T(8,128)}, f32[40,8,144]{2,1,0:T(8,128)S(1)}, u32[]{:S(2)}) copy-start(f32[40,8,144]{2,1,0:T(8,128)S(1)} %collective-permute-done.2) | copy-start | bytes 552964
  63.0 0.7 copy-start.2
  67.0 9.0 %collective-permute-start.4 = (f32[40,64,8]{1,2,0:T(8,128)S(1)}, f32[40,64,8]{1,2,0:T(8,128)}, u32[]{:S(2)}, u32[]{:S(2)}) collective-permute-start(f32[40,64,8]{1,2,0:T(8,128)S(1)} %copy.84), channel_id=1, source_target_pairs={{0,1},{1,2},{2,3},{3,0},{4,5},{5,6},{6,7},{7,4},{8,9},{9,10},{10,1... | collective-permute-start | bytes 245768 | tf_op jit(solution)/shard_map/ppermute | solution.py:24
  69.6 9.1 %collective-permute-start.5 = (f32[40,64,8]{1,2,0:T(8,128)}, f32[40,64,8]{1,2,0:T(8,128)}, u32[]{:S(2)}, u32[]{:S(2)}) collective-permute-start(f32[40,64,8]{1,2,0:T(8,128)} %copy.85), channel_id=1, source_target_pairs={{1,0},{2,1},{3,2},{0,3},{5,4},{6,5},{7,6},{4,7},{9,8},{10,9},{11,1... | collective-permute-start | bytes 245768 | tf_op jit(solution)/shard_map/ppermute | solution.py:27
  85.2 15.8 %copy-start.3 = (f32[8,32,128]{2,1,0:T(8,128)}, f32[8,32,128]{2,1,0:T(8,128)S(1)}, u32[]{:S(2)}) copy-start(f32[8,32,128]{2,1,0:T(8,128)S(1)} %scatter-add.19) | copy-start | bytes 393220
  86.0 10.3 %all-to-all-start.2 = ((f32[8,32,128]{2,0,1:T(8,128)}), f32[8,32,128]{2,0,1:T(8,128)S(1)}, u32[]{:S(2)}, u32[]{:S(2)}) async-start(f32[8,32,128]{2,0,1:T(8,128)} %copy.88), calls=%async_computation.2 | async-start | bytes 262144 | tf_op jit(solution)/shard_map/all_to_all | solution.py:129
where the time goes:
time: 140 us; the launch traced here: 139 us
  waiting for transfers between devices  29.1 us (21%)
  matrix products  27.9 us (20%)
  blocking collectives  24.2 us (17%)
  starting transfers between devices  20.9 us (15%)
  local copies, waits for them, and re-layouts  19.1 us (14%)
  other arithmetic  16.8 us (12%)
    ppermute x3, waiting for transfers between devices, padded_2(): lax.ppermute(lax.slice_in_dim(block, block.shape[dim] - width, None, axis...  15.1 us
    all_to_all x1, blocking collectives, shards(): lax.all_to_all(lax.all_to_all(split_view, 'gy', split_axis=5, concat_axis...  12.2 us
    all_to_all x1, blocking collectives, shards(): lax.all_to_all(section_y, 'gx', split_axis=2, concat_axis=3, tiled=True)  8.11 us
    dot_general x3, matrix products, planes(): return jnp.einsum('sjb,sjac->abc', along_y, mixed_planes, precision=highest)  7.98 us
    ppermute x3, waiting for transfers between devices, padded_2(): lax.ppermute(lax.slice_in_dim(block, 0, width, axis=dim), axis, backward)  7.02 us
    dot_general x3, matrix products, planes(): jnp.einsum('sia,sijc->sjac', group_x, partial_z, precision=highest)  6.84 us
    all_to_all x1, starting transfers between devices, shards(): lax.all_to_all(routed_labels, 'gx', split_axis=1, concat_axis=1, tiled=True)  5.19 us
    dot_general x1, matrix products, shards(): imag_z = -jnp.einsum('xyz,zk->xyk', depth_local, sine_z, precision=highest)  4.78 us
  transfers between devices with their start and end apart: 9, of which 9 were waited for; matrix products, arithmetic and copies ran while one was open for 8% of the time, Pallas kernels for 0%

commit v1 on v0

v1 whole, which is shorter than its diff:
```python
import functools
import math

import numpy as np
import jax
import jax.numpy as jnp
from jax import lax
from jax.experimental import pallas as pl
from jax.experimental.pallas import tpu as pltpu
from jax.sharding import PartitionSpec as P

DEG = 3
HALO = 8
CX = 8
CY = 32
CZ = 128
SIDE = DEG + 1
EXTRA = 8

highest = lax.Precision.HIGHEST
high = lax.Precision.HIGH


def lanes_dot(a, b):
    return lax.dot_general(
        a, b, (((1,), (1,)), ((), ())), precision=high, preferred_element_type=jnp.float32
    )


def plain_dot(a, b):
    return lax.dot_general(
        a, b, (((1,), (0,)), ((), ())), precision=high, preferred_element_type=jnp.float32
    )


def pack_kernel(table, basis, blocks, cells, offsets, exponent_index, radius_index, out):
    npoly = basis.shape[0]
    out[0:npoly, :] = lanes_dot(basis[...], blocks[...])
    radius = (HALO - radius_index[...]).astype(jnp.float32)
    chosen = exponent_index[...]
    value = jnp.zeros(chosen.shape, jnp.float32)
    for row in range(table.shape[0]):
        value = jnp.where(chosen == row, table[row], value)
    out[npoly : npoly + 3, :] = cells[...].astype(jnp.float32)
    out[npoly + 3 : npoly + 6, :] = offsets[...]
    out[npoly + 6 : npoly + 7, :] = value / (radius * radius)
    out[npoly + 7 : npoly + 8, :] = radius


def factor_rows(coordinate, cell, offset, rate, radius, period):
    steps = coordinate - cell
    if period is not None:
        half = period / 2.0
        steps = jnp.where(steps > half, steps - period, steps)
        steps = jnp.where(steps < -half, steps + period, steps)
    distance = steps - offset
    envelope = jnp.exp(-rate * distance * distance)
    envelope = jnp.where(jnp.abs(steps) <= radius, envelope, 0.0)
    scaled = distance / HALO
    rows = [envelope]
    for degree in range(DEG):
        rows.append(rows[-1] * scaled)
    return rows


def collocate_kernel(anchor, pieces, out, *, period_x, period_y):
    npoly = SIDE**3
    joined = jnp.concatenate([pieces[b] for b in range(pieces.shape[0])], axis=1)
    count = joined.shape[1]

    def row(index):
        return joined[index : index + 1, :]

    rate = row(npoly + 6)
    radius = row(npoly + 7)

    def coordinates(extent, start):
        index = lax.broadcasted_iota(jnp.int32, (extent, count), 0)
        return (index + start).astype(jnp.float32)

    extent_z = CZ + 2 * HALO
    along_x = factor_rows(
        coordinates(CX, anchor[0]), row(npoly), row(npoly + 3), rate, radius, period_x
    )
    along_y = factor_rows(
        coordinates(CY, anchor[1]), row(npoly + 1), row(npoly + 4), rate, radius, period_y
    )
    along_z = factor_rows(
        coordinates(extent_z, anchor[2] - HALO), row(npoly + 2), row(npoly + 5), rate, radius, None
    )
    y_all = jnp.concatenate(along_y, axis=1)
    total = None
    for i in range(SIDE):
        mixed = []
        for j in range(SIDE):
            part = None
            for k in range(SIDE):
                term = along_z[k] * row((i * SIDE + j) * SIDE + k)
                part = term if part is None else part + term
            mixed.append(part)
        x_all = jnp.concatenate([along_x[i]] * SIDE, axis=1)
        outer = (x_all[:, None, :] * y_all[None, :, :]).reshape(CX * CY, SIDE * count)
        product = lanes_dot(outer, jnp.concatenate(mixed, axis=1))
        total = product if total is None else total + product
    total = total.reshape(CX, CY, extent_z)

    @pl.when(pl.program_id(0) == 0)
    def first():
        out[...] = total

    @pl.when(pl.program_id(0) != 0)
    def later():
        out[...] += total


def swap_parts(values, half):
    width = 2 * half
    tiles = []
    for t in range(values.shape[1] // width):
        tiles.append(pltpu.roll(values[:, t * width : (t + 1) * width], half, 1))
    swapped = jnp.concatenate(tiles, axis=1) if len(tiles) > 1 else tiles[0]
    lane = lax.broadcasted_iota(jnp.int32, values.shape, 1) % width
    return jnp.where(lane < half, swapped, -swapped)


def plane_kernel(pieces, table_z, table_y, out, *, groups_y, groups_z, half):
    total = None
    for g in range(groups_z):
        rows = jnp.concatenate([pieces[r * groups_z + g] for r in range(groups_y)], axis=0)
        product = plain_dot(rows, table_z[g])
        total = product if total is None else total + product
    both = jnp.concatenate([total, swap_parts(total, half)], axis=0)
    result = plain_dot(table_y[...], both)
    groups_x, chunks, ky, width = out.shape
    for g in range(groups_x):
        for c in range(chunks):
            out[g, c] = result[g * ky : (g + 1) * ky, c * width : (c + 1) * width]


def lines_kernel(pieces, table_x, out, *, half):
    ky = pieces.shape[1]
    width = 2 * half
    values = jnp.concatenate([pieces[:, q, :] for q in range(ky)], axis=1)
    both = jnp.concatenate([values, swap_parts(values, half)], axis=0)
    result = plain_dot(table_x[...], both)
    for q in range(ky):
        out[0, q] = result[:, q * width : q * width + half]
        out[1, q] = result[:, q * width + half : (q + 1) * width]


def vmem_call(kernel, shape):
    return pl.pallas_call(kernel, out_shape=jax.ShapeDtypeStruct(shape, jnp.float32))


def angle_parts(rows, columns, length):
    product = (rows[:, None].astype(np.int64) * columns[None, :]) % length
    angles = product.astype(np.float64) * (2.0 * math.pi / length)
    factor = 1.0 / math.sqrt(length)
    return np.cos(angles) * factor, np.sin(angles) * factor


def pair_table(length):
    index = np.arange(length)
    cosine, sine = angle_parts(index, index, length)
    return np.concatenate([cosine, sine], axis=1).astype(np.float32)


def depth_table(groups, length, chunk):
    cells = (np.arange(groups)[:, None] * CZ - HALO + np.arange(CZ + 2 * HALO)[None, :]) % length
    cosine, sine = angle_parts(cells.reshape(-1), np.arange(length), length)
    both = np.stack(
        [cosine.reshape(-1, length // chunk, chunk), -sine.reshape(-1, length // chunk, chunk)], 2
    )
    return both.reshape(groups, CZ + 2 * HALO, 2 * length).astype(np.float32)


def dft_parts(length):
    indices = jnp.arange(length, dtype=jnp.int32)
    product = indices[:, None] * indices[None, :] % length
    angles = product.astype(jnp.float32) * (2.0 * math.pi / length)
    factor = 1.0 / math.sqrt(length)
    return (jnp.cos(angles) * factor, jnp.sin(angles) * factor)


def shifts(count):
    forward = [(i, (i + 1) % count) for i in range(count)]
    backward = [(target, source) for source, target in forward]
    return forward, backward


def spectrum_by_axes(density):
    depth_local = lax.all_to_all(density, "gz", split_axis=1, concat_axis=2, tiled=True)
    depth_size = depth_local.shape[2]
    cosine_z, sine_z = dft_parts(depth_size)
    real_z = jnp.einsum("xyz,zk->xyk", depth_local, cosine_z, precision=highest)
    imag_z = -jnp.einsum("xyz,zk->xyk", depth_local, sine_z, precision=highest)
    section_z = jnp.stack([real_z, imag_z])
    rows_devices = lax.axis_size("gy")
    depth_devices = lax.axis_size("gz")
    depth_piece = depth_size // (rows_devices * depth_devices)
    split_view = section_z.reshape(
        2, CX, 1, 1, section_z.shape[2], rows_devices, depth_devices, depth_piece
    )
    moved_rows = lax.all_to_all(
        lax.all_to_all(split_view, "gy", split_axis=5, concat_axis=2, tiled=True),
        "gz",
        split_axis=6,
        concat_axis=3,
        tiled=True,
    )
    rows_local = moved_rows.reshape(2, CX, -1, depth_piece)
    cosine_y, sine_y = dft_parts(rows_local.shape[2])
    real_in = rows_local[0]
    imag_in = rows_local[1]
    real_y = jnp.einsum("xyk,yl->klx", real_in, cosine_y, precision=highest) + jnp.einsum(
        "xyk,yl->klx", imag_in, sine_y, precision=highest
    )
    imag_y = jnp.einsum("xyk,yl->klx", imag_in, cosine_y, precision=highest) - jnp.einsum(
        "xyk,yl->klx", real_in, sine_y, precision=highest
    )
    section_y = jnp.stack([real_y, imag_y])
    width_local = lax.all_to_all(section_y, "gx", split_axis=2, concat_axis=3, tiled=True)
    cosine_x, sine_x = dft_parts(width_local.shape[3])
    real_w = width_local[0]
    imag_w = width_local[1]
    real_x = jnp.einsum("kyx,xm->kym", real_w, cosine_x, precision=highest) + jnp.einsum(
        "kyx,xm->kym", imag_w, sine_x, precision=highest
    )
    imag_x = jnp.einsum("kyx,xm->kym", imag_w, cosine_x, precision=highest) - jnp.einsum(
        "kyx,xm->kym", real_w, sine_x, precision=highest
    )
    return jnp.stack([real_x, imag_x])


def spectrum_by_planes(extended):
    groups_x = lax.axis_size("gx")
    groups_y = lax.axis_size("gy")
    groups_z = lax.axis_size("gz")
    chunks = groups_y * groups_z
    size_x, size_y, size_z = groups_x * CX, groups_y * CY, groups_z * CZ
    half = size_z // chunks
    ky = size_y // groups_x
    planes = lax.all_to_all(extended, ("gy", "gz"), 0, 0, tiled=True)
    sent = vmem_call(
        functools.partial(plane_kernel, groups_y=groups_y, groups_z=groups_z, half=half),
        (groups_x, chunks, ky, 2 * half),
    )(planes, depth_table(groups_z, size_z, half), pair_table(size_y))
    lines = lax.all_to_all(
        sent.reshape(groups_x * chunks, ky, 2 * half), ("gx", "gy", "gz"), 0, 0, tiled=True
    )
    result = vmem_call(functools.partial(lines_kernel, half=half), (2, ky, size_x, half))(
        lines, pair_table(size_x)
    )
    return jnp.transpose(result, (0, 3, 1, 2))


def shards(
    pair_blocks, basis_map, pair_cells, pair_offsets, exponent_index, radius_index, exponents
):
    pair_dev = pair_blocks.shape[1]
    npoly = basis_map.shape[1]
    groups_x = lax.axis_size("gx")
    groups_y = lax.axis_size("gy")
    groups_z = lax.axis_size("gz")
    in_vmem = pl.BlockSpec(memory_space=pltpu.VMEM)
    packed = pl.pallas_call(
        pack_kernel,
        out_shape=jax.ShapeDtypeStruct((npoly + EXTRA, pair_dev), jnp.float32),
        in_specs=[pl.BlockSpec(memory_space=pltpu.SMEM)] + [in_vmem] * 6,
    )(
        exponents,
        basis_map.T,
        pair_blocks.T,
        pair_cells,
        pair_offsets,
        exponent_index[None, :],
        radius_index[None, :],
    )
    if groups_y <= 2:
        gathered = lax.all_gather(packed, ("gx", "gy"))
    else:
        column = lax.all_gather(packed, "gx")
        forward, backward = shifts(groups_y)
        gathered = jnp.concatenate(
            [column, lax.ppermute(column, "gy", forward), lax.ppermute(column, "gy", backward)], 0
        )
    blocks = gathered.shape[0]
    step = 8 if blocks % 8 == 0 else blocks
    anchor = jnp.stack(
        [lax.axis_index("gx") * CX, lax.axis_index("gy") * CY, lax.axis_index("gz") * CZ]
    ).astype(jnp.int32)
    extent_z = CZ + 2 * HALO
    extended = pl.pallas_call(
        functools.partial(
            collocate_kernel, period_x=float(groups_x * CX), period_y=float(groups_y * CY)
        ),
        out_shape=jax.ShapeDtypeStruct((CX, CY, extent_z), jnp.float32),
        grid=(blocks // step,),
        in_specs=[
            pl.BlockSpec(memory_space=pltpu.SMEM),
            pl.BlockSpec((step, npoly + EXTRA, pair_dev), lambda g: (g, 0, 0)),
        ],
        out_specs=pl.BlockSpec((CX, CY, extent_z), lambda g: (0, 0, 0)),
    )(anchor, gathered)
    forward, backward = shifts(groups_z)
    below = lax.ppermute(extended[:, :, CZ + HALO :], "gz", forward)
    above = lax.ppermute(extended[:, :, :HALO], "gz", backward)
    density = (
        extended[:, :, HALO : HALO + CZ]
        + jnp.pad(below, ((0, 0), (0, 0), (0, CZ - HALO)))
        + jnp.pad(above, ((0, 0), (0, 0), (CZ - HALO, 0)))
    )
    chunks = groups_y * groups_z
    aligned = CX == chunks and (2 * groups_z * CZ // chunks) % 128 == 0
    aligned = aligned and (groups_y * CY // groups_x) % 8 == 0
    spectrum = spectrum_by_planes(extended) if aligned else spectrum_by_axes(density)
    return (density, spectrum)


def solution(mesh):
    placed = (
        P(None, ("gx", "gy", "gz")),
        P(),
        P(None, ("gx", "gy", "gz")),
        P(None, ("gx", "gy", "gz")),
        P(("gx", "gy", "gz")),
        P(("gx", "gy", "gz")),
        P(),
    )
    return jax.shard_map(
        shards,
        mesh=mesh,
        in_specs=placed,
        out_specs=(P("gx", "gy", "gz"), P(None, ("gy", "gz"), "gx", None)),
        check_vma=False,
    )
```

time: 140 us -> 56.4 us (0.40)
  matrix products: 27.9 us -> 0 us
  waiting for transfers between devices: 29.1 us -> 8.6 us
  local copies, waits for them, and re-layouts: 19.1 us -> 2.48 us
  other arithmetic: 16.8 us -> 1.42 us
  starting transfers between devices: 20.9 us -> 6.46 us
  Pallas kernels: 0 us -> 11.1 us
    dot_general x19 -> x0, matrix products: 27.9 us -> none  [the longest x3 7.98 us: planes(): return jnp.einsum('sjb,sjac->abc', along_y, mixed_planes, precision=highest)]
    ppermute x6 -> x2, waiting for transfers between devices: 22.1 us -> 8.6 us  [the longest x1 8.3 us: shards(): below = lax.ppermute(extended[:, :, CZ + HALO:], 'gz', forward)]
    pallas_call x0 -> x4, Pallas kernels: none -> 11.1 us  [the longest x1 3.8 us: shards(): pl.pallas_call(functools.partial(collocate_kernel, period_x=float(groups_...]
    all_to_all x3 -> x1, starting transfers between devices: 13.5 us -> 2.59 us  [spectrum_by_planes(): lax.all_to_all(sent.reshape(groups_x * chunks, ky, 2 * half), ('gx', 'gy'...]
    all_gather x0 -> x1, blocking collectives: none -> 10.7 us  [shards(): gathered = lax.all_gather(packed, ('gx', 'gy'))]
    all_to_all x3 -> x1, blocking collectives: 24.2 us -> 14.5 us  [spectrum_by_planes(): planes = lax.all_to_all(extended, ('gy', 'gz'), 0, 0, tiled=True)]
    all_to_all x3 -> x1, waiting for transfers between devices: 7.02 us -> 0.01 us  [spectrum_by_planes(): lax.all_to_all(sent.reshape(groups_x * chunks, ky, 2 * half), ('gx', 'gy'...]
    slice x10 -> x1, local copies, waits for them, and re-layouts: 4.53 us -> 0.09 us  [shards(): below = lax.ppermute(extended[:, :, CZ + HALO:], 'gz', forward)]
  transfers between devices with their start and end apart: 9 -> 3, of which waited for: 9 -> 2; matrix products, arithmetic and copies ran while one was open for 8% -> 2% of each run, Pallas kernels for 0% -> 0%
where the time goes in v1:
time: 56.4 us; the launch traced here: 55.9 us
  blocking collectives  25.2 us (45%)
  Pallas kernels  11.1 us (20%)
  waiting for transfers between devices  8.6 us (15%)
  starting transfers between devices  6.46 us (11%)
  local copies, waits for them, and re-layouts  2.48 us (4%)
  other arithmetic  1.42 us (3%)
  between operations  0.67 us (1%)
    all_to_all x1, blocking collectives, spectrum_by_planes(): planes = lax.all_to_all(extended, ('gy', 'gz'), 0, 0, tiled=True)  14.5 us
    all_gather x1, blocking collectives, shards(): gathered = lax.all_gather(packed, ('gx', 'gy'))  10.7 us
    ppermute x1, waiting for transfers between devices, shards(): below = lax.ppermute(extended[:, :, CZ + HALO:], 'gz', forward)  8.3 us
    pallas_call x1, Pallas kernels, shards(): pl.pallas_call(functools.partial(collocate_kernel, period_x=float(groups_...  3.8 us
    pallas_call x1, Pallas kernels, spectrum_by_planes(): vmem_call(functools.partial(plane_kernel, groups_y=groups_y, groups_z=gro...  3.31 us
    all_to_all x1, starting transfers between devices, spectrum_by_planes(): lax.all_to_all(sent.reshape(groups_x * chunks, ky, 2 * half), ('gx', 'gy'...  2.59 us
    pallas_call x1, Pallas kernels, spectrum_by_planes(): vmem_call(functools.partial(lines_kernel, half=half), (2, ky, size_x, half))  2.2 us
    ppermute x1, starting transfers between devices, shards(): above = lax.ppermute(extended[:, :, :HALO], 'gz', backward)  2.14 us
  transfers between devices with their start and end apart: 3, of which 2 were waited for; matrix products, arithmetic and copies ran while one was open for 2% of the time, Pallas kernels for 0%

profile of v1, /device:TPU:0, one launch (start us, length us, event | category | flops | bytes accessed | tf_op | source)
XLA Modules:
  0.0 55.9 jit_solution(14755374561818594000)
XLA Ops:
  0.6 1.8 %shard_map.113 = f32[72,32]{1,0:T(8,128)} custom-call(f32[16]{0:T(128)} %table.1, f32[64,529]{1,0:T(8,128)} %bitcast.12, f32[32,529]{1,0:T(8,128)} %bitcast.14, s32[3,32]{1,0:T(4,128)} %cells.1, f32[3,32]{1,0:T(4,128)} %offsets.1, s32[1,32]{1,0:T(1,128)} %bitcast.15, s32[1,32]{1,0:T(1,128)} %bitcast.16), custom_call_target="tpu_custom_call" | custom-call | tf_op jit(solution)/shard_map/pallas_call | solution.py:266
  2.5 0.8 %copy.12 = f32[1,72,32]{1,2,0:T(8,128)S(1)} copy(f32[1,72,32]{2,1,0:T(8,128)} %bitcast.13) | data formatting | bytes 18432
  3.3 10.7 %all-gather.1 = f32[8,72,32]{1,2,0:T(8,128)S(1)} all-gather(f32[1,72,32]{1,2,0:T(8,128)S(1)} %copy.12), channel_id=2, replica_groups=mesh['gx'=4,'gy'=2,'gz'=4] {'gx','gy'}, dimensions={0}, use_global_device_ids=true | all-gather | bytes 82944 | tf_op jit(solution)/shard_map/all_gather | solution.py:280
  14.0 0.9 %copy.13.pieces = f32[8,72,32]{2,1,0:T(8,128)} copy(f32[8,72,32]{1,2,0:T(8,128)S(1)} %all-gather.1) | data formatting | bytes 147456 | tf_op jit(solution)/shard_map/all_gather | solution.py:280
  14.8 0.6 %pad_add_fusion.anchor = s32[3]{0:T(128)} fusion(s32[1]{0:T(128)} %bitcast.2, s32[1]{0:T(128)} %bitcast.1, s32[1]{0:T(128)} %bitcast), kind=kLoop, calls=%fused_computation.2 | loop fusion | flops 6 | bytes 24 | tf_op jit(solution)/shard_map/stack | solution.py:289
  15.5 3.8 %shard_map.114 = f32[8,32,144]{2,1,0:T(8,128)} custom-call(s32[3]{0:T(128)} %pad_add_fusion.anchor, f32[8,72,32]{2,1,0:T(8,128)} %copy.13.pieces), custom_call_target="tpu_custom_call" | custom-call | tf_op jit(solution)/shard_map/pallas_call | solution.py:293
  19.3 0.0 copy-start
  19.3 14.5 %all_to_all.10.pieces = f32[8,32,144]{2,1,0:T(8,128)} all-to-all(f32[8,32,144]{2,1,0:T(8,128)} %shard_map.114), channel_id=1, replica_groups=mesh['gx'=4,'gy'=2,'gz'=4] {'gy','gz'}, dimensions={0} | all-to-all | bytes 294912 | tf_op jit(solution)/shard_map/all_to_all | solution.py:243
  33.7 3.3 %shard_map.115 = f32[4,8,16,128]{3,2,1,0:T(8,128)} custom-call(f32[8,32,144]{2,1,0:T(8,128)} %all_to_all.10.pieces, f32[4,144,1024]{2,1,0:T(8,128)} %constant.27.clone.table_z, f32[64,128]{1,0:T(8,128)} %constant.28.clone.table_y), custom_call_target="tpu_custom_call" | custom-call | tf_op jit(solution)/shard_map/pallas_call | solution.py:244
  37.0 2.6 %all-to-all-start.1 = ((f32[32,16,128]{2,1,0:T(8,128)}), f32[32,16,128]{2,1,0:T(8,128)S(1)}, u32[]{:S(2)}, u32[]{:S(2)}) async-start(f32[32,16,128]{2,1,0:T(8,128)} %bitcast.10), calls=%async_computation.1 | async-start | bytes 524288 | tf_op jit(solution)/shard_map/all_to_all | solution.py:248
  39.6 0.0 copy-done
  39.7 0.1 fusion.1
  39.7 1.7 %collective-permute-start = (f32[8,32,8]{2,1,0:T(8,128)S(1)}, f32[8,32,8]{2,1,0:T(8,128)S(1)}, u32[]{:S(2)}, u32[]{:S(2)}) collective-permute-start(f32[8,32,8]{2,1,0:T(8,128)S(1)} %get-tuple-element.2), channel_id=1, source_target_pairs={{0,1},{1,2},{2,3},{3,0},{4,5},{5,6},{6,7},{7,4},{8,9},{9,10},{10,1... | collective-permute-start | bytes 24584 | tf_op jit(solution)/shard_map/ppermute | solution.py:306
  41.5 2.1 %collective-permute-start.1 = (f32[8,32,8]{2,1,0:T(8,128)S(1)}, f32[8,32,8]{2,1,0:T(8,128)S(1)}, u32[]{:S(2)}, u32[]{:S(2)}) collective-permute-start(f32[8,32,8]{2,1,0:T(8,128)S(1)} %get-tuple-element.3), channel_id=1, source_target_pairs={{1,0},{2,1},{3,2},{0,3},{5,4},{6,5},{7,6},{4,7},{9,8},{10,9},{11,1... | collective-permute-start | bytes 24584 | tf_op jit(solution)/shard_map/ppermute | solution.py:307
  43.6 8.3 %collective-permute-done = f32[8,32,8]{2,1,0:T(8,128)S(1)} collective-permute-done((f32[8,32,8]{2,1,0:T(8,128)S(1)}, f32[8,32,8]{2,1,0:T(8,128)S(1)}, u32[]{:S(2)}, u32[]{:S(2)}) %collective-permute-start) | collective-permute-done | bytes 8224 | tf_op jit(solution)/shard_map/ppermute | solution.py:306
  51.9 0.3 collective-permute-done.1
  52.2 0.8 %fusion = f32[8,32,128]{2,1,0:T(8,128)} fusion(f32[8,32,144]{2,1,0:T(8,128)S(1)} %copy-done, f32[8,32,8]{2,1,0:T(8,128)S(1)} %collective-permute-done.1, f32[8,32,8]{2,1,0:T(8,128)S(1)} %collective-permute-done), kind=kLoop, calls=%fused_computation.1 | loop fusion | flops 65536 | bytes 278528 | tf_op jit(solution)/shard_map/add | solution.py:309
  53.0 0.0 all-to-all-done.1.pieces
  53.0 0.0 copy-start.1
  53.0 0.7 %copy-done.1 = f32[32,16,128]{2,1,0:T(8,128)} copy-done((f32[32,16,128]{2,1,0:T(8,128)}, f32[32,16,128]{2,1,0:T(8,128)S(1)}, u32[]{:S(2)}) %copy-start.1) | copy-done | bytes 262168
  53.7 2.2 %shard_map.116 = f32[2,16,32,64]{3,2,1,0:T(8,128)} custom-call(f32[32,16,128]{2,1,0:T(8,128)} %copy-done.1, f32[32,64]{1,0:T(8,128)} %constant.29.clone.table_x), custom_call_target="tpu_custom_call" | custom-call | tf_op jit(solution)/shard_map/pallas_call | solution.py:251
Async XLA Ops:
  19.3 20.4 %copy-start = (f32[8,32,144]{2,1,0:T(8,128)S(1)}, f32[8,32,144]{2,1,0:T(8,128)}, u32[]{:S(2)}) copy-start(f32[8,32,144]{2,1,0:T(8,128)} %shard_map.114) | copy-start | bytes 442372
  37.0 16.0 %all-to-all-start.1 = ((f32[32,16,128]{2,1,0:T(8,128)}), f32[32,16,128]{2,1,0:T(8,128)S(1)}, u32[]{:S(2)}, u32[]{:S(2)}) async-start(f32[32,16,128]{2,1,0:T(8,128)} %bitcast.10), calls=%async_computation.1 | async-start | bytes 524288 | tf_op jit(solution)/shard_map/all_to_all | solution.py:248
  39.7 12.2 %collective-permute-start = (f32[8,32,8]{2,1,0:T(8,128)S(1)}, f32[8,32,8]{2,1,0:T(8,128)S(1)}, u32[]{:S(2)}, u32[]{:S(2)}) collective-permute-start(f32[8,32,8]{2,1,0:T(8,128)S(1)} %get-tuple-element.2), channel_id=1, source_target_pairs={{0,1},{1,2},{2,3},{3,0},{4,5},{5,6},{6,7},{7,4},{8,9},{9,10},{10,1... | collective-permute-start | bytes 24584 | tf_op jit(solution)/shard_map/ppermute | solution.py:306
  41.5 10.7 %collective-permute-start.1 = (f32[8,32,8]{2,1,0:T(8,128)S(1)}, f32[8,32,8]{2,1,0:T(8,128)S(1)}, u32[]{:S(2)}, u32[]{:S(2)}) collective-permute-start(f32[8,32,8]{2,1,0:T(8,128)S(1)} %get-tuple-element.3), channel_id=1, source_target_pairs={{1,0},{2,1},{3,2},{0,3},{5,4},{6,5},{7,6},{4,7},{9,8},{10,9},{11,1... | collective-permute-start | bytes 24584 | tf_op jit(solution)/shard_map/ppermute | solution.py:307
  53.0 0.7 %copy-start.1 = (f32[32,16,128]{2,1,0:T(8,128)}, f32[32,16,128]{2,1,0:T(8,128)S(1)}, u32[]{:S(2)}) copy-start(f32[32,16,128]{2,1,0:T(8,128)S(1)} %all-to-all-done.1.pieces) | copy-start | bytes 786436

commit v2 on v1

--- a/solution.py
+++ b/solution.py
@@ -34,17 +34,33 @@
 
 
 def pack_kernel(table, basis, blocks, cells, offsets, exponent_index, radius_index, out):
-    npoly = basis.shape[0]
-    out[0:npoly, :] = lanes_dot(basis[...], blocks[...])
+    coefficients = lanes_dot(basis[...], blocks[...])
     radius = (HALO - radius_index[...]).astype(jnp.float32)
     chosen = exponent_index[...]
     value = jnp.zeros(chosen.shape, jnp.float32)
     for row in range(table.shape[0]):
         value = jnp.where(chosen == row, table[row], value)
-    out[npoly : npoly + 3, :] = cells[...].astype(jnp.float32)
-    out[npoly + 3 : npoly + 6, :] = offsets[...]
-    out[npoly + 6 : npoly + 7, :] = value / (radius * radius)
-    out[npoly + 7 : npoly + 8, :] = radius
+    values = jnp.concatenate(
+        [
+            coefficients,
+            cells[...].astype(jnp.float32),
+            offsets[...],
+            value / (radius * radius),
+            radius,
+        ],
+        axis=0,
+    )
+    if len(out.shape) == 2:
+        out[...] = values
+    else:
+        copies, rows, width = out.shape
+        count = values.shape[1]
+        groups = values.shape[0] // rows
+        spare = [jnp.zeros((rows, width - groups * count), jnp.float32)]
+        parts = [values[g * rows : (g + 1) * rows] for g in range(groups)]
+        dense = jnp.concatenate(parts + (spare if width > groups * count else []), axis=1)
+        for c in range(copies):
+            out[c] = dense
 
 
 def factor_rows(coordinate, cell, offset, rate, radius, period):
@@ -113,6 +129,89 @@
         out[...] += total
 
 
+def joined_pairs(pieces, sources, count):
+    rows = pieces.shape[1]
+    groups = (SIDE**3 + EXTRA) // rows
+    loaded = [pieces[source] for source in sources]
+    return jnp.concatenate(
+        [
+            jnp.concatenate([part[:, g * count : (g + 1) * count] for part in loaded], axis=1)
+            for g in range(groups)
+        ],
+        axis=0,
+    )
+
+
+def cell_range(start, extent, count):
+    index = lax.broadcasted_iota(jnp.int32, (extent, count), 0)
+    return (index + start).astype(jnp.float32)
+
+
+def along(joined, axis, coordinate, period):
+    base = SIDE**3
+
+    def row(index):
+        return joined[base + index : base + index + 1, :]
+
+    return factor_rows(coordinate, row(axis), row(3 + axis), row(6), row(7), period)
+
+
+def weighted(along_z, joined, first):
+    part = None
+    for k in range(SIDE):
+        term = along_z[k] * joined[first + k : first + k + 1, :]
+        part = term if part is None else part + term
+    return part
+
+
+def group_sources(groups_x, groups_y, groups_z, group):
+    return [(x * groups_y + y) * groups_z + group for x in range(groups_x) for y in range(groups_y)]
+
+
+def block_kernel(anchor, pieces, out, *, groups, count):
+    groups_x, groups_y, groups_z = groups
+    period_x, period_y = float(groups_x * CX), float(groups_y * CY)
+    own = anchor[2]
+
+    def load(group):
+        joined = joined_pairs(pieces, group_sources(groups_x, groups_y, groups_z, group), count)
+        lanes = joined.shape[1]
+        along_x = along(joined, 0, cell_range(anchor[0] * CX, CX, lanes), period_x)
+        along_y = along(joined, 1, cell_range(anchor[1] * CY, CY, lanes), period_y)
+        return joined, lanes, along_x, jnp.concatenate(along_y, axis=1)
+
+    joined, lanes, along_x, y_all = load(own)
+    along_z = along(joined, 2, cell_range(own * CZ, CZ, lanes), None)
+    total = None
+    for i in range(SIDE):
+        mixed = [weighted(along_z, joined, (i * SIDE + j) * SIDE) for j in range(SIDE)]
+        x_all = jnp.concatenate([along_x[i]] * SIDE, axis=1)
+        outer = (x_all[:, None, :] * y_all[None, :, :]).reshape(CX * CY, SIDE * lanes)
+        product = lanes_dot(outer, jnp.concatenate(mixed, axis=1))
+        total = product if total is None else total + product
+    out[...] = total.reshape(CX, CY, CZ)
+
+    def rim(group, first_cell, place):
+        joined, lanes, along_x, y_all = load(group)
+        along_z = along(joined, 2, cell_range(first_cell, HALO, lanes), None)
+        columns = []
+        for j in range(SIDE):
+            column = None
+            for i in range(SIDE):
+                mixed = weighted(along_z, joined, (i * SIDE + j) * SIDE)
+                term = along_x[i][:, None, :] * mixed[None, :, :]
+                column = term if column is None else column + term
+            columns.append(column.reshape(CX * HALO, lanes))
+        product = lanes_dot(y_all, jnp.concatenate(columns, axis=1))
+        for x in range(CX):
+            out[x, :, place : place + HALO] += product[:, x * HALO : (x + 1) * HALO]
+
+    before = (own + groups_z - 1) % groups_z
+    after = (own + 1) % groups_z
+    rim(before, (before + 1) * CZ, 0)
+    rim(after, after * CZ - HALO, CZ - HALO)
+
+
 def swap_parts(values, half):
     width = 2 * half
     tiles = []
@@ -123,18 +222,33 @@
     return jnp.where(lane < half, swapped, -swapped)
 
 
-def plane_kernel(pieces, table_z, table_y, out, *, groups_y, groups_z, half):
+def plane_kernel(anchor, pieces, table_z, table_y, out, *, groups, count, half):
+    groups_x, groups_y, groups_z = groups
+    period_x, period_y = float(groups_x * CX), float(groups_y * CY)
+    plane = anchor[0] * CX + anchor[1] * groups_z + anchor[2]
     total = None
     for g in range(groups_z):
-        rows = jnp.concatenate([pieces[r * groups_z + g] for r in range(groups_y)], axis=0)
+        joined = joined_pairs(pieces, group_sources(groups_x, groups_y, groups_z, g), count)
+        lanes = joined.shape[1]
+        along_x = along(joined, 0, cell_range(plane, 1, lanes), period_x)
+        along_y = along(joined, 1, cell_range(0, groups_y * CY, lanes), period_y)
+        along_z = along(joined, 2, cell_range(g * CZ - HALO, CZ + 2 * HALO, lanes), None)
+        square = SIDE * SIDE
+        crossed = None
+        for i in range(SIDE):
+            term = along_x[i] * joined[i * square : (i + 1) * square, :]
+            crossed = term if crossed is None else crossed + term
+        mixed = [weighted(along_z, crossed, j * SIDE) for j in range(SIDE)]
+        rows = lanes_dot(jnp.concatenate(along_y, axis=1), jnp.concatenate(mixed, axis=1))
         product = plain_dot(rows, table_z[g])
         total = product if total is None else total + product
     both = jnp.concatenate([total, swap_parts(total, half)], axis=0)
     result = plain_dot(table_y[...], both)
-    groups_x, chunks, ky, width = out.shape
+    ky, width = out.shape[1:]
+    chunks = groups_y * groups_z
     for g in range(groups_x):
         for c in range(chunks):
-            out[g, c] = result[g * ky : (g + 1) * ky, c * width : (c + 1) * width]
+            out[g * chunks + c] = result[g * ky : (g + 1) * ky, c * width : (c + 1) * width]
 
 
 def lines_kernel(pieces, table_x, out, *, half):
@@ -148,8 +262,13 @@
         out[1, q] = result[:, q * width + half : (q + 1) * width]
 
 
-def vmem_call(kernel, shape):
-    return pl.pallas_call(kernel, out_shape=jax.ShapeDtypeStruct(shape, jnp.float32))
+def vmem_call(kernel, shape, spaces):
+    return pl.pallas_call(
+        kernel,
+        out_shape=jax.ShapeDtypeStruct(shape, jnp.float32),
+        in_specs=[pl.BlockSpec(memory_space=space) for space in spaces],
+        out_specs=pl.BlockSpec(memory_space=pltpu.VMEM),
+    )
 
 
 def angle_parts(rows, columns, length):
@@ -232,26 +351,31 @@
     return jnp.stack([real_x, imag_x])
 
 
-def spectrum_by_planes(extended):
-    groups_x = lax.axis_size("gx")
-    groups_y = lax.axis_size("gy")
-    groups_z = lax.axis_size("gz")
+def by_planes(pack, groups, pair_dev, anchor):
+    groups_x, groups_y, groups_z = groups
     chunks = groups_y * groups_z
     size_x, size_y, size_z = groups_x * CX, groups_y * CY, groups_z * CZ
     half = size_z // chunks
     ky = size_y // groups_x
-    planes = lax.all_to_all(extended, ("gy", "gz"), 0, 0, tiled=True)
+    everyone = ("gx", "gy", "gz")
+    dense = pack((groups_x * chunks, (SIDE**3 + EXTRA) // 3, 128))
+    gathered = lax.all_to_all(dense, everyone, 0, 0, tiled=True)
+    smem, vmem = pltpu.SMEM, pltpu.VMEM
     sent = vmem_call(
-        functools.partial(plane_kernel, groups_y=groups_y, groups_z=groups_z, half=half),
-        (groups_x, chunks, ky, 2 * half),
-    )(planes, depth_table(groups_z, size_z, half), pair_table(size_y))
-    lines = lax.all_to_all(
-        sent.reshape(groups_x * chunks, ky, 2 * half), ("gx", "gy", "gz"), 0, 0, tiled=True
-    )
-    result = vmem_call(functools.partial(lines_kernel, half=half), (2, ky, size_x, half))(
-        lines, pair_table(size_x)
-    )
-    return jnp.transpose(result, (0, 3, 1, 2))
+        functools.partial(plane_kernel, groups=groups, count=pair_dev, half=half),
+        (groups_x * chunks, ky, 2 * half),
+        [smem] + [vmem] * 3,
+    )(anchor, gathered, depth_table(groups_z, size_z, half), pair_table(size_y))
+    lines = lax.all_to_all(sent, everyone, 0, 0, tiled=True)
+    density = vmem_call(
+        functools.partial(block_kernel, groups=groups, count=pair_dev),
+        (CX, CY, CZ),
+        [smem, vmem],
+    )(anchor, gathered)
+    result = vmem_call(
+        functools.partial(lines_kernel, half=half), (2, ky, size_x, half), [vmem] * 2
+    )(lines, pair_table(size_x))
+    return density, jnp.transpose(result, (0, 3, 1, 2))
 
 
 def shards(
@@ -262,20 +386,24 @@
     groups_x = lax.axis_size("gx")
     groups_y = lax.axis_size("gy")
     groups_z = lax.axis_size("gz")
-    in_vmem = pl.BlockSpec(memory_space=pltpu.VMEM)
-    packed = pl.pallas_call(
-        pack_kernel,
-        out_shape=jax.ShapeDtypeStruct((npoly + EXTRA, pair_dev), jnp.float32),
-        in_specs=[pl.BlockSpec(memory_space=pltpu.SMEM)] + [in_vmem] * 6,
-    )(
-        exponents,
-        basis_map.T,
-        pair_blocks.T,
-        pair_cells,
-        pair_offsets,
-        exponent_index[None, :],
-        radius_index[None, :],
-    )
+    def pack(shape):
+        return vmem_call(pack_kernel, shape, [pltpu.SMEM] + [pltpu.VMEM] * 6)(
+            exponents,
+            basis_map.T,
+            pair_blocks.T,
+            pair_cells,
+            pair_offsets,
+            exponent_index[None, :],
+            radius_index[None, :],
+        )
+
+    chunks = groups_y * groups_z
+    aligned = CX == chunks and 2 * groups_z * CZ == 128 * chunks and 3 * pair_dev <= 128
+    if aligned and (groups_y * CY // groups_x) % 8 == 0:
+        place = jnp.stack([lax.axis_index(name) for name in ("gx", "gy", "gz")])
+        sizes = (groups_x, groups_y, groups_z)
+        return by_planes(pack, sizes, pair_dev, place.astype(jnp.int32))
+    packed = pack((npoly + EXTRA, pair_dev))
     if groups_y <= 2:
         gathered = lax.all_gather(packed, ("gx", "gy"))
     else:
@@ -310,10 +438,7 @@
         + jnp.pad(below, ((0, 0), (0, 0), (0, CZ - HALO)))
         + jnp.pad(above, ((0, 0), (0, 0), (CZ - HALO, 0)))
     )
-    chunks = groups_y * groups_z
-    aligned = CX == chunks and (2 * groups_z * CZ // chunks) % 128 == 0
-    aligned = aligned and (groups_y * CY // groups_x) % 8 == 0
-    spectrum = spectrum_by_planes(extended) if aligned else spectrum_by_axes(density)
+    spectrum = spectrum_by_axes(density)
     return (density, spectrum)
 
 

time: 56.4 us -> 45.6 us (0.81)
  blocking collectives: 25.2 us -> 0 us
  waiting for transfers between devices: 8.6 us -> 17.3 us
  starting transfers between devices: 6.46 us -> 11.1 us
  Pallas kernels: 11.1 us -> 14.1 us
  local copies, waits for them, and re-layouts: 2.48 us -> 1.44 us
  other arithmetic: 1.42 us -> 0.6 us
    all_to_all x1 -> x2, waiting for transfers between devices: 0.01 us -> 17.3 us  [the longest x1 11.2 us: by_planes(): gathered = lax.all_to_all(dense, everyone, 0, 0, tiled=True)]
    all_to_all x1 -> x0, blocking collectives: 14.5 us -> none  [spectrum_by_planes(): planes = lax.all_to_all(extended, ('gy', 'gz'), 0, 0, tiled=True)]
    all_gather x1 -> x0, blocking collectives: 10.7 us -> none  [shards(): gathered = lax.all_gather(packed, ('gx', 'gy'))]
    ppermute x2 -> x0, waiting for transfers between devices: 8.6 us -> none  [the longest x1 8.3 us: shards(): below = lax.ppermute(extended[:, :, CZ + HALO:], 'gz', forward)]
    all_to_all x1 -> x2, starting transfers between devices: 2.59 us -> 11.1 us  [the longest x1 7.32 us: by_planes(): gathered = lax.all_to_all(dense, everyone, 0, 0, tiled=True)]
    ppermute x2 -> x0, starting transfers between devices: 3.88 us -> none  [the longest x1 2.14 us: shards(): above = lax.ppermute(extended[:, :, :HALO], 'gz', backward)]
    pallas_call x4, Pallas kernels: 11.1 us -> 14.1 us  [the longest x1 5.7 us: by_planes(): vmem_call(functools.partial(plane_kernel, groups=groups, count=pair_dev,...]
    all_gather x1 -> x0, local copies, waits for them, and re-layouts: 0.86 us -> none  [shards(): gathered = lax.all_gather(packed, ('gx', 'gy'))]
  transfers between devices with their start and end apart: 3 -> 2, of which waited for: 2 -> 2; matrix products, arithmetic and copies ran while one was open for 2% -> 1% of each run, Pallas kernels for 0% -> 9%
where the time goes in v2:
time: 45.6 us; the launch traced here: 45.2 us
  waiting for transfers between devices  17.3 us (38%)
  Pallas kernels  14.1 us (31%)
  starting transfers between devices  11.1 us (24%)
  local copies, waits for them, and re-layouts  1.44 us (3%)
  between operations  0.66 us (1%)
  other arithmetic  0.6 us (1%)
    all_to_all x1, waiting for transfers between devices, by_planes(): gathered = lax.all_to_all(dense, everyone, 0, 0, tiled=True)  11.2 us
    all_to_all x1, starting transfers between devices, by_planes(): gathered = lax.all_to_all(dense, everyone, 0, 0, tiled=True)  7.32 us
    all_to_all x1, waiting for transfers between devices, by_planes(): lines = lax.all_to_all(sent, everyone, 0, 0, tiled=True)  6.03 us
    pallas_call x1, Pallas kernels, by_planes(): vmem_call(functools.partial(plane_kernel, groups=groups, count=pair_dev,...  5.7 us
    pallas_call x1, Pallas kernels, by_planes(): vmem_call(functools.partial(block_kernel, groups=groups, count=pair_dev),...  4.2 us
    all_to_all x1, starting transfers between devices, by_planes(): lines = lax.all_to_all(sent, everyone, 0, 0, tiled=True)  3.81 us
    pallas_call x1, Pallas kernels, by_planes(): vmem_call(functools.partial(lines_kernel, half=half), (2, ky, size_x, hal...  2.2 us
    pallas_call x1, Pallas kernels, pack(): vmem_call(pack_kernel, shape, [pltpu.SMEM] + [pltpu.VMEM] * 6)  2.04 us
  transfers between devices with their start and end apart: 2, of which 2 were waited for; matrix products, arithmetic and copies ran while one was open for 1% of the time, Pallas kernels for 9%

profile of v2, /device:TPU:0, one launch (start us, length us, event | category | flops | bytes accessed | tf_op | source)
XLA Modules:
  0.0 45.2 jit_solution(8662132897253115125)
XLA Ops:
  0.6 2.0 %shard_map.113 = f32[32,24,128]{2,1,0:T(8,128)} custom-call(f32[16]{0:T(128)} %table.1, f32[64,529]{1,0:T(8,128)} %bitcast.9, f32[32,529]{1,0:T(8,128)} %bitcast.10, s32[3,32]{1,0:T(4,128)} %cells.1, f32[3,32]{1,0:T(4,128)} %offsets.1, s32[1,32]{1,0:T(1,128)} %bitcast.11, s32[1,32]{1,0:T(1,128)} %bitcast.12), custom_call_target="tpu_custom_call" | custom-call | tf_op jit(solution)/shard_map/pallas_call | solution.py:390
  2.7 7.3 %all-to-all-start = ((f32[32,24,128]{2,1,0:T(8,128)}), f32[32,24,128]{2,1,0:T(8,128)S(1)}, u32[]{:S(2)}, u32[]{:S(2)}) async-start(f32[32,24,128]{2,1,0:T(8,128)} %shard_map.113), calls=%async_computation | async-start | bytes 786432 | tf_op jit(solution)/shard_map/all_to_all | solution.py:362
  10.0 0.6 %pad_add_fusion.anchor = s32[3]{0:T(128)} fusion(s32[1]{0:T(128)} %bitcast.2, s32[1]{0:T(128)} %bitcast.1, s32[1]{0:T(128)} %bitcast), kind=kLoop, calls=%fused_computation | loop fusion | flops 6 | bytes 24 | tf_op jit(solution)/shard_map/stack | solution.py:403
  10.6 11.2 %all-to-all-done.pieces = f32[32,24,128]{2,1,0:T(8,128)S(1)} async-done(((f32[32,24,128]{2,1,0:T(8,128)}), f32[32,24,128]{2,1,0:T(8,128)S(1)}, u32[]{:S(2)}, u32[]{:S(2)}) %all-to-all-start) | async-done | bytes 393248 | tf_op jit(solution)/shard_map/all_to_all | solution.py:362
  21.8 0.0 copy-start
  21.9 0.7 %copy-done = f32[32,24,128]{2,1,0:T(8,128)} copy-done((f32[32,24,128]{2,1,0:T(8,128)}, f32[32,24,128]{2,1,0:T(8,128)S(1)}, u32[]{:S(2)}) %copy-start) | copy-done | bytes 393240
  22.6 5.7 %shard_map.115 = f32[32,16,128]{2,1,0:T(8,128)} custom-call(s32[3]{0:T(128)} %pad_add_fusion.anchor, f32[32,24,128]{2,1,0:T(8,128)} %copy-done, f32[4,144,1024]{2,1,0:T(8,128)} %constant.18.clone.table_z, f32[64,128]{1,0:T(8,128)} %constant.19.clone.table_y), custom_call_target="tpu_custom_call" | custom-call | tf_op jit(solution)/shard_map/pallas_call | solution.py:364
  28.3 3.8 %all-to-all-start.1 = ((f32[32,16,128]{2,1,0:T(8,128)}), f32[32,16,128]{2,1,0:T(8,128)S(1)}, u32[]{:S(2)}, u32[]{:S(2)}) async-start(f32[32,16,128]{2,1,0:T(8,128)} %shard_map.115), calls=%async_computation.1 | async-start | bytes 524288 | tf_op jit(solution)/shard_map/all_to_all | solution.py:369
  32.1 4.2 %shard_map.114 = f32[8,32,128]{2,1,0:T(8,128)} custom-call(s32[3]{0:T(128)} %pad_add_fusion.anchor, f32[32,24,128]{2,1,0:T(8,128)} %copy-done), custom_call_target="tpu_custom_call" | custom-call | tf_op jit(solution)/shard_map/pallas_call | solution.py:370
  36.3 6.0 %all-to-all-done.1.pieces = f32[32,16,128]{2,1,0:T(8,128)S(1)} async-done(((f32[32,16,128]{2,1,0:T(8,128)}), f32[32,16,128]{2,1,0:T(8,128)S(1)}, u32[]{:S(2)}, u32[]{:S(2)}) %all-to-all-start.1) | async-done | bytes 262176 | tf_op jit(solution)/shard_map/all_to_all | solution.py:369
  42.3 0.0 copy-start.1
  42.3 0.7 %copy-done.1 = f32[32,16,128]{2,1,0:T(8,128)} copy-done((f32[32,16,128]{2,1,0:T(8,128)}, f32[32,16,128]{2,1,0:T(8,128)S(1)}, u32[]{:S(2)}) %copy-start.1) | copy-done | bytes 262168
  43.0 2.2 %shard_map.116 = f32[2,16,32,64]{3,2,1,0:T(8,128)} custom-call(f32[32,16,128]{2,1,0:T(8,128)} %copy-done.1, f32[32,64]{1,0:T(8,128)} %constant.20.clone.table_x), custom_call_target="tpu_custom_call" | custom-call | tf_op jit(solution)/shard_map/pallas_call | solution.py:375
Async XLA Ops:
  2.7 19.2 %all-to-all-start = ((f32[32,24,128]{2,1,0:T(8,128)}), f32[32,24,128]{2,1,0:T(8,128)S(1)}, u32[]{:S(2)}, u32[]{:S(2)}) async-start(f32[32,24,128]{2,1,0:T(8,128)} %shard_map.113), calls=%async_computation | async-start | bytes 786432 | tf_op jit(solution)/shard_map/all_to_all | solution.py:362
  21.8 0.7 %copy-start = (f32[32,24,128]{2,1,0:T(8,128)}, f32[32,24,128]{2,1,0:T(8,128)S(1)}, u32[]{:S(2)}) copy-start(f32[32,24,128]{2,1,0:T(8,128)S(1)} %all-to-all-done.pieces) | copy-start | bytes 1179652
  28.3 14.0 %all-to-all-start.1 = ((f32[32,16,128]{2,1,0:T(8,128)}), f32[32,16,128]{2,1,0:T(8,128)S(1)}, u32[]{:S(2)}, u32[]{:S(2)}) async-start(f32[32,16,128]{2,1,0:T(8,128)} %shard_map.115), calls=%async_computation.1 | async-start | bytes 524288 | tf_op jit(solution)/shard_map/all_to_all | solution.py:369
  42.3 0.7 %copy-start.1 = (f32[32,16,128]{2,1,0:T(8,128)}, f32[32,16,128]{2,1,0:T(8,128)S(1)}, u32[]{:S(2)}) copy-start(f32[32,16,128]{2,1,0:T(8,128)S(1)} %all-to-all-done.1.pieces) | copy-start | bytes 786436

commit v3 on v2

--- a/solution.py
+++ b/solution.py
@@ -222,11 +222,22 @@
     return jnp.where(lane < half, swapped, -swapped)
 
 
-def plane_kernel(anchor, pieces, table_z, table_y, out, *, groups, count, half):
+def plane_kernel(
+    anchor, far_pieces, far_upper, far_lower, table_y, out,
+    pieces, upper, lower, sem_pieces, sem_upper, sem_lower, *, groups, count, half
+):
+    fetch = pltpu.make_async_copy(far_pieces, pieces, sem_pieces)
+    fetch.start()
+    fetch_upper = pltpu.make_async_copy(far_upper, upper, sem_upper)
+    fetch_upper.start()
+    fetch_lower = pltpu.make_async_copy(far_lower, lower, sem_lower)
+    fetch_lower.start()
+    fetch.wait()
     groups_x, groups_y, groups_z = groups
     period_x, period_y = float(groups_x * CX), float(groups_y * CY)
     plane = anchor[0] * CX + anchor[1] * groups_z + anchor[2]
     total = None
+    parts = []
     for g in range(groups_z):
         joined = joined_pairs(pieces, group_sources(groups_x, groups_y, groups_z, g), count)
         lanes = joined.shape[1]
@@ -240,7 +251,14 @@
             crossed = term if crossed is None else crossed + term
         mixed = [weighted(along_z, crossed, j * SIDE) for j in range(SIDE)]
         rows = lanes_dot(jnp.concatenate(along_y, axis=1), jnp.concatenate(mixed, axis=1))
-        product = plain_dot(rows, table_z[g])
+        parts.append(split_bf16(rows))
+    fetch_upper.wait()
+    fetch_lower.wait()
+    for g in range(groups_z):
+        rows_upper, rows_lower = parts[g]
+        product = bf16_dot(rows_upper, upper[g]) + (
+            bf16_dot(rows_upper, lower[g]) + bf16_dot(rows_lower, upper[g])
+        )
         total = product if total is None else total + product
     both = jnp.concatenate([total, swap_parts(total, half)], axis=0)
     result = plain_dot(table_y[...], both)
@@ -260,6 +278,27 @@
     for q in range(ky):
         out[0, q] = result[:, q * width : q * width + half]
         out[1, q] = result[:, q * width + half : (q + 1) * width]
+
+
+def split_bf16(values):
+    upper = values.astype(jnp.bfloat16)
+    lower = (values - upper.astype(jnp.float32)).astype(jnp.bfloat16)
+    return upper, lower
+
+
+def bf16_dot(a, b):
+    return lax.dot_general(a, b, (((1,), (0,)), ((), ())), preferred_element_type=jnp.float32)
+
+
+def staged_call(kernel, shape, spaces, scratch):
+    copies = [pltpu.SemaphoreType.DMA(()) for _ in scratch]
+    return pl.pallas_call(
+        kernel,
+        out_shape=jax.ShapeDtypeStruct(shape, jnp.float32),
+        in_specs=[pl.BlockSpec(memory_space=space) for space in spaces],
+        out_specs=pl.BlockSpec(memory_space=pltpu.VMEM),
+        scratch_shapes=[pltpu.VMEM(array.shape, array.dtype) for array in scratch] + copies,
+    )
 
 
 def vmem_call(kernel, shape, spaces):
@@ -360,12 +399,16 @@
     everyone = ("gx", "gy", "gz")
     dense = pack((groups_x * chunks, (SIDE**3 + EXTRA) // 3, 128))
     gathered = lax.all_to_all(dense, everyone, 0, 0, tiled=True)
-    smem, vmem = pltpu.SMEM, pltpu.VMEM
-    sent = vmem_call(
+    smem, vmem, free = pltpu.SMEM, pltpu.VMEM, pl.ANY
+    table = depth_table(groups_z, size_z, half)
+    upper = table.astype(jnp.bfloat16)
+    lower = (table - upper.astype(np.float32)).astype(jnp.bfloat16)
+    sent = staged_call(
         functools.partial(plane_kernel, groups=groups, count=pair_dev, half=half),
         (groups_x * chunks, ky, 2 * half),
-        [smem] + [vmem] * 3,
-    )(anchor, gathered, depth_table(groups_z, size_z, half), pair_table(size_y))
+        [smem, free, free, free, vmem],
+        [gathered, upper, lower],
+    )(anchor, gathered, upper, lower, pair_table(size_y))
     lines = lax.all_to_all(sent, everyone, 0, 0, tiled=True)
     density = vmem_call(
         functools.partial(block_kernel, groups=groups, count=pair_dev),

time: 45.6 us -> 45.4 us (level)
  no operation moved by 1% of the time
where the time goes in v3:
time: 45.4 us; the launch traced here: 45 us
  waiting for transfers between devices  17.3 us (38%)
  Pallas kernels  13.9 us (31%)
  starting transfers between devices  11.1 us (24%)
  local copies, waits for them, and re-layouts  1.44 us (3%)
  between operations  0.67 us (1%)
  other arithmetic  0.6 us (1%)
    all_to_all x1, waiting for transfers between devices, by_planes(): gathered = lax.all_to_all(dense, everyone, 0, 0, tiled=True)  11.2 us
    all_to_all x1, starting transfers between devices, by_planes(): gathered = lax.all_to_all(dense, everyone, 0, 0, tiled=True)  7.32 us
    all_to_all x1, waiting for transfers between devices, by_planes(): lines = lax.all_to_all(sent, everyone, 0, 0, tiled=True)  6.03 us
    pallas_call x1, Pallas kernels, by_planes(): staged_call(functools.partial(plane_kernel, groups=groups, count=pair_dev...  5.45 us
    pallas_call x1, Pallas kernels, by_planes(): vmem_call(functools.partial(block_kernel, groups=groups, count=pair_dev),...  4.2 us
    all_to_all x1, starting transfers between devices, by_planes(): lines = lax.all_to_all(sent, everyone, 0, 0, tiled=True)  3.82 us
    pallas_call x1, Pallas kernels, by_planes(): vmem_call(functools.partial(lines_kernel, half=half), (2, ky, size_x, hal...  2.2 us
    pallas_call x1, Pallas kernels, pack(): vmem_call(pack_kernel, shape, [pltpu.SMEM] + [pltpu.VMEM] * 6)  2.04 us
  transfers between devices with their start and end apart: 2, of which 2 were waited for; matrix products, arithmetic and copies ran while one was open for 1% of the time, Pallas kernels for 9%

profile of v3, /device:TPU:0, one launch (start us, length us, event | category | flops | bytes accessed | tf_op | source)
XLA Modules:
  0.0 45.0 jit_solution(5005745932558063980)
XLA Ops:
  0.6 2.0 %shard_map.122 = f32[32,24,128]{2,1,0:T(8,128)} custom-call(f32[16]{0:T(128)} %table.1, f32[64,529]{1,0:T(8,128)} %bitcast.9, f32[32,529]{1,0:T(8,128)} %bitcast.10, s32[3,32]{1,0:T(4,128)} %cells.1, f32[3,32]{1,0:T(4,128)} %offsets.1, s32[1,32]{1,0:T(1,128)} %bitcast.11, s32[1,32]{1,0:T(1,128)} %bitcast.12), custom_call_target="tpu_custom_call" | custom-call | tf_op jit(solution)/shard_map/pallas_call | solution.py:433
  2.7 7.3 %all-to-all-start = ((f32[32,24,128]{2,1,0:T(8,128)}), f32[32,24,128]{2,1,0:T(8,128)S(1)}, u32[]{:S(2)}, u32[]{:S(2)}) async-start(f32[32,24,128]{2,1,0:T(8,128)} %shard_map.122), calls=%async_computation | async-start | bytes 786432 | tf_op jit(solution)/shard_map/all_to_all | solution.py:401
  10.0 0.6 %pad_add_fusion.anchor = s32[3]{0:T(128)} fusion(s32[1]{0:T(128)} %bitcast.2, s32[1]{0:T(128)} %bitcast.1, s32[1]{0:T(128)} %bitcast), kind=kLoop, calls=%fused_computation | loop fusion | flops 6 | bytes 24 | tf_op jit(solution)/shard_map/stack | solution.py:446
  10.6 11.2 %all-to-all-done.pieces.far_pieces = f32[32,24,128]{2,1,0:T(8,128)S(1)} async-done(((f32[32,24,128]{2,1,0:T(8,128)}), f32[32,24,128]{2,1,0:T(8,128)S(1)}, u32[]{:S(2)}, u32[]{:S(2)}) %all-to-all-start) | async-done | bytes 393248 | tf_op jit(solution)/shard_map/all_to_all | solution.py:401
  21.8 0.0 copy-start
  21.9 0.7 %copy-done = f32[32,24,128]{2,1,0:T(8,128)} copy-done((f32[32,24,128]{2,1,0:T(8,128)}, f32[32,24,128]{2,1,0:T(8,128)S(1)}, u32[]{:S(2)}) %copy-start) | copy-done | bytes 393240
  22.6 5.4 %shard_map.124 = f32[32,16,128]{2,1,0:T(8,128)} custom-call(s32[3]{0:T(128)} %pad_add_fusion.anchor, f32[32,24,128]{2,1,0:T(8,128)} %copy-done, bf16[4,144,1024]{2,1,0:T(8,128)(2,1)} %constant.20.clone.far_upper, bf16[4,144,1024]{2,1,0:T(8,128)(2,1)} %constant.21.clone.far_lower, f32[64,128]{1,0:T(8,128)} %constant.22.clone.table_y), custom_call_target="tpu_custom_call" | custom-call | tf_op jit(solution)/shard_map/pallas_call | solution.py:406
  28.1 3.8 %all-to-all-start.1 = ((f32[32,16,128]{2,1,0:T(8,128)}), f32[32,16,128]{2,1,0:T(8,128)S(1)}, u32[]{:S(2)}, u32[]{:S(2)}) async-start(f32[32,16,128]{2,1,0:T(8,128)} %shard_map.124), calls=%async_computation.1 | async-start | bytes 524288 | tf_op jit(solution)/shard_map/all_to_all | solution.py:412
  31.9 4.2 %shard_map.123 = f32[8,32,128]{2,1,0:T(8,128)} custom-call(s32[3]{0:T(128)} %pad_add_fusion.anchor, f32[32,24,128]{2,1,0:T(8,128)} %copy-done), custom_call_target="tpu_custom_call" | custom-call | tf_op jit(solution)/shard_map/pallas_call | solution.py:413
  36.1 6.0 %all-to-all-done.1.pieces = f32[32,16,128]{2,1,0:T(8,128)S(1)} async-done(((f32[32,16,128]{2,1,0:T(8,128)}), f32[32,16,128]{2,1,0:T(8,128)S(1)}, u32[]{:S(2)}, u32[]{:S(2)}) %all-to-all-start.1) | async-done | bytes 262176 | tf_op jit(solution)/shard_map/all_to_all | solution.py:412
  42.1 0.0 copy-start.1
  42.1 0.7 %copy-done.1 = f32[32,16,128]{2,1,0:T(8,128)} copy-done((f32[32,16,128]{2,1,0:T(8,128)}, f32[32,16,128]{2,1,0:T(8,128)S(1)}, u32[]{:S(2)}) %copy-start.1) | copy-done | bytes 262168
  42.8 2.2 %shard_map.125 = f32[2,16,32,64]{3,2,1,0:T(8,128)} custom-call(f32[32,16,128]{2,1,0:T(8,128)} %copy-done.1, f32[32,64]{1,0:T(8,128)} %constant.23.clone.table_x), custom_call_target="tpu_custom_call" | custom-call | tf_op jit(solution)/shard_map/pallas_call | solution.py:418
Async XLA Ops:
  2.7 19.2 %all-to-all-start = ((f32[32,24,128]{2,1,0:T(8,128)}), f32[32,24,128]{2,1,0:T(8,128)S(1)}, u32[]{:S(2)}, u32[]{:S(2)}) async-start(f32[32,24,128]{2,1,0:T(8,128)} %shard_map.122), calls=%async_computation | async-start | bytes 786432 | tf_op jit(solution)/shard_map/all_to_all | solution.py:401
  21.8 0.7 %copy-start = (f32[32,24,128]{2,1,0:T(8,128)}, f32[32,24,128]{2,1,0:T(8,128)S(1)}, u32[]{:S(2)}) copy-start(f32[32,24,128]{2,1,0:T(8,128)S(1)} %all-to-all-done.pieces.far_pieces) | copy-start | bytes 1179652
  28.1 14.1 %all-to-all-start.1 = ((f32[32,16,128]{2,1,0:T(8,128)}), f32[32,16,128]{2,1,0:T(8,128)S(1)}, u32[]{:S(2)}, u32[]{:S(2)}) async-start(f32[32,16,128]{2,1,0:T(8,128)} %shard_map.124), calls=%async_computation.1 | async-start | bytes 524288 | tf_op jit(solution)/shard_map/all_to_all | solution.py:412
  42.1 0.7 %copy-start.1 = (f32[32,16,128]{2,1,0:T(8,128)}, f32[32,16,128]{2,1,0:T(8,128)S(1)}, u32[]{:S(2)}) copy-start(f32[32,16,128]{2,1,0:T(8,128)S(1)} %all-to-all-done.1.pieces) | copy-start | bytes 786436
